TPU v7x, 32 devices: a whole 2x2x4 slice. The times are simulated.
32 devices in a mesh: blk: 4 (over z), tok: 8 (over y, x, core).
Axes of the slice: x: 2, y: 2, z: 4, core: 2. Of those that a mesh axis runs over, the one named last changes fastest.
Arguments:
- inputs: float32 [2048, 16384], P('tok', 'blk'), may hold values from -6 to 6
- first_factor: float32 [16, 1024, 1024], P('blk', 'tok'), may hold values from -0.1875 to 0.1875
- second_factor: float32 [16, 1024, 1024], P('blk', 'tok'), may hold values from -0.1875 to 0.1875
- cotangent: float32 [2048, 16384], P('tok', 'blk'), may hold values from -6 to 6
Outputs:
- input_grad: float32 [2048, 16384], P('tok', 'blk')
- first_grad: float32 [16, 1024, 1024], P('blk', 'tok')
- second_grad: float32 [16, 1024, 1024], P('blk', 'tok')
All inputs are finite; a program needn't handle non-finite values.
Results may differ from a plain program's by a relative error of at most 0.00013.
Values sent between devices are 32-bit elements; how exact they have to be, the bound alone decides.
No kernel may reach another device: no remote copies, remote signals or barrier semaphores. Data moves between devices by JAX's collectives and lax.ppermute only.
A program may use at most 128 MiB of HBM per device.

v0:
```python
import math

import jax
import jax.numpy as jnp
from jax import lax
from jax.sharding import PartitionSpec as P


def body(inputs, first_factor, second_factor, cotangent):
    hp = lax.Precision.HIGHEST
    local_blocks = first_factor.shape[0]
    order = first_factor.shape[2]
    blocks = local_blocks * lax.axis_size("blk")
    group = order // blocks
    count = inputs.shape[0]
    xb = inputs.reshape(count, local_blocks, order)
    first_whole, second_whole = (
        lax.all_gather(first_factor, "tok", axis=1, tiled=True),
        lax.all_gather(second_factor, "tok", axis=1, tiled=True),
    )
    first_view = first_whole.reshape(local_blocks, order, blocks, group)
    first = jnp.einsum("tbi,bisg->stbg", xb, first_view, precision=hp).reshape(
        blocks, count, local_blocks * group
    )
    mixed = lax.all_to_all(first, "blk", split_axis=0, concat_axis=2, tiled=True)
    second = jnp.einsum("btk,bko->tbo", mixed, second_whole, precision=hp)
    normal_cdf = 0.5 * (1.0 + jax.scipy.special.erf(second / math.sqrt(2.0)))
    density = jnp.exp(-0.5 * second * second) / math.sqrt(2.0 * math.pi)
    delta_second = cotangent.reshape(count, local_blocks, order) * (normal_cdf + second * density)
    second_grad = jnp.einsum("btk,tbo->bko", mixed, delta_second, precision=hp)
    second_out = lax.psum_scatter(second_grad, "tok", scatter_dimension=1, tiled=True)
    delta_mixed = jnp.einsum("tbo,bko->btk", delta_second, second_whole, precision=hp)
    delta_first = lax.all_to_all(delta_mixed, "blk", split_axis=2, concat_axis=0, tiled=True)
    delta_view = delta_first.reshape(blocks, count, local_blocks, group)
    first_grad = jnp.einsum("tbi,stbg->bisg", xb, delta_view, precision=hp).reshape(
        local_blocks, order, order
    )
    input_grad = jnp.einsum("stbg,bisg->tbi", delta_view, first_view, precision=hp).reshape(
        count, local_blocks * order
    )
    first_out = lax.psum_scatter(first_grad, "tok", scatter_dimension=1, tiled=True)
    return (input_grad, first_out, second_out)


def solution(mesh):
    placed = (P("tok", "blk"), P("blk", "tok", None), P("blk", "tok", None), P("tok", "blk"))
    return jax.shard_map(
        body,
        mesh=mesh,
        in_specs=placed,
        out_specs=(P("tok", "blk"), P("blk", "tok", None), P("blk", "tok", None)),
        check_vma=False,
    )
```

profile of v0, /device:TPU:0, one launch (start us, length us, event | category | flops | bytes accessed | tf_op | source)
XLA Modules:
  0.0 574.9 jit_solution(17563923800015692502)
XLA Ops:
  7.2 0.0 all-gather.3.cloned.1.call-start
  7.2 0.7 all-gather.3.cloned.1.call-update
  7.9 0.0 all-gather.5.cloned.1.call-start
  7.9 0.7 all-gather.5.cloned.1.call-update
  8.6 6.1 %reshape.30 = f32[256,4,1024]{2,1,0:T(4,128)} reshape(f32[256,4096]{1,0:T(8,128)} %param.4) | data formatting | bytes 8388608 | tf_op jit(solution)/shard_map/reshape | solution.py:16
  14.7 87.6 %all-gather.3.cloned.1.call-done = f32[4,1024,1024]{2,1,0:T(8,128)} async-done(((f32[4,128,1024]{2,1,0:T(8,128)}), f32[4,1024,1024]{2,1,0:T(8,128)}) %all-gather.3.cloned.1.call-update) | async-done | bytes 16777232 | tf_op jit(solution)/shard_map/all_gather | solution.py:18
  102.4 16.8 %copy.43 = f32[4,1024,1024]{1,2,0:T(8,128)} copy(f32[4,1024,1024]{2,1,0:T(8,128)} %all-gather.3.cloned.1.call-done) | data formatting | bytes 33554432 | tf_op jit(solution)/shard_map/all_gather | solution.py:18
  119.1 20.6 %fusion.15 = f32[16,256,4,64]{1,3,0,2:T(8,128)S(1)} fusion(f32[4,1024,16,64]{1,3,2,0:T(8,128)} %bitcast.41, f32[256,4,1024,1]{2,1,0,3:T(4,128)} %bitcast.44), kind=kOutput, calls=%fused_computation.17 | convolution fusion | flops 12884901888 | bytes 25165824 | tf_op jit(solution)/shard_map/tbi,bisg->stbg/dot_general | solution.py:22
  139.7 2.4 copy.45
  142.2 5.2 all-to-all-start
  147.4 0.2 reduce-scatter.5.cloned.1.call-start
  147.6 5.6 copy.42
  153.2 5.5 copy.48
  158.6 82.6 %all-to-all-done = f32[16,256,256]{1,2,0:T(8,128)} async-done(((f32[16,256,256]{1,2,0:T(8,128)}), f32[16,256,256]{1,2,0:T(8,128)}, u32[]{:S(2)}, u32[]{:S(2)}) %all-to-all-start) | async-done | bytes 4194336 | tf_op jit(solution)/shard_map/all_to_all | solution.py:25
  241.2 5.2 copy.47
  246.4 5.8 %all_to_all.27 = f32[4,256,1024]{2,1,0:T(8,128)} reshape(f32[4,256,4,256]{3,2,1,0:T(4,128)} %copy.47) | data formatting | bytes 8388608 | tf_op jit(solution)/shard_map/all_to_all | solution.py:25
  252.2 21.3 %fusion.6 = f32[256,4,1024]{2,0,1:T(8,128)S(1)} fusion(f32[256,4,1024]{2,0,1:T(8,128)} %copy.48, f32[4,256,1024]{2,1,0:T(8,128)} %all_to_all.27, f32[4,1024,1024]{2,1,0:T(8,128)} %all-gather.5.cloned.1.call-done), kind=kOutput, calls=%fused_computation.7 | convolution fusion | flops 12894339072 | bytes 29360128 | tf_op jit(solution)/shard_map/btk,bko->tbo/dot_general | solution.py:26
  273.5 2.0 copy-done
  275.5 16.6 %fusion.22 = f32[4,1024,1024]{2,1,0:T(8,128)} fusion(f32[4,256,1024]{2,1,0:T(8,128)S(1)} %copy-done.1, f32[256,4,1024]{2,0,1:T(8,128)S(1)} %fusion.6), kind=kOutput, calls=%fused_computation.20 | convolution fusion | flops 12884901888 | bytes 25165824 | tf_op jit(solution)/shard_map/btk,tbo->bko/dot_general | solution.py:30
  292.2 0.0 reduce-scatter.3.cloned.1.call-start
  292.2 20.2 %fusion.21 = f32[4,256,1024]{2,1,0:T(8,128)} fusion(f32[256,4,1024]{2,0,1:T(8,128)} %copy-done, f32[4,1024,1024]{2,1,0:T(8,128)} %all-gather.5.cloned.1.call-done), kind=kOutput, calls=%fused_computation.19 | convolution fusion | flops 12884901888 | bytes 25165824 | tf_op jit(solution)/shard_map/tbo,bko->btk/dot_general | solution.py:32
  312.4 5.7 copy.49
  318.1 96.6 %all_to_all.33 = f32[4,256,1024]{1,0,2:T(4,128)S(1)} all-to-all(f32[4,256,1024]{1,0,2:T(4,128)} %copy.49), channel_id=1, replica_groups=mesh['blk'=4,'tok'=8] {'blk'}, dimensions={2} | all-to-all | bytes 8388608 | tf_op jit(solution)/shard_map/all_to_all | solution.py:33
  414.7 0.8 copy.50
  415.5 0.4 copy.51
  415.9 3.3 copy-done.2
  419.2 17.7 %fusion.10 = f32[4,16,64,1024]{3,2,1,0:T(8,128)} fusion(f32[16,256,4,64]{1,3,2,0:T(8,128)S(1)} %bitcast.50, f32[256,4,1024,1]{2,1,0,3:T(4,128)S(1)} %bitcast.45), kind=kOutput, calls=%fused_computation.12 | convolution fusion | flops 12884901888 | bytes 25165824 | tf_op jit(solution)/shard_map/tbi,stbg->bisg/dot_general | solution.py:35
  436.9 16.4 %copy.56 = f32[4,1024,1024]{2,1,0:T(8,128)} copy(f32[4,1024,1024]{1,2,0:T(8,128)} %bitcast.43) | data formatting | bytes 33554432 | tf_op jit(solution)/shard_map/reshape | solution.py:35
  453.3 20.1 %fusion.18 = f32[256,4,1024]{2,0,1:T(8,128)} fusion(f32[16,256,4,64]{1,3,2,0:T(8,128)} %bitcast.51, f32[4,1024,16,64]{1,3,2,0:T(8,128)} %bitcast.42), kind=kOutput, calls=%fused_computation.18 | convolution fusion | flops 12884901888 | bytes 25165824 | tf_op jit(solution)/shard_map/stbg,bisg->tbi/dot_general | solution.py:38
  473.4 6.0 %copy.53 = f32[256,4,1024]{0,2,1:T(8,128)} copy(f32[256,4,1024]{2,0,1:T(8,128)} %fusion.18) | data formatting | bytes 8388608 | tf_op jit(solution)/shard_map/stbg,bisg->tbi/transpose | solution.py:38
  479.4 5.7 copy.58
  485.1 82.9 %reduce-scatter.3.cloned.1.call-done = f32[4,128,1024]{2,1,0:T(8,128)} async-done(((f32[4,1024,1024]{2,1,0:T(8,128)}), f32[4,128,1024]{2,1,0:T(8,128)}) %reduce-scatter.3.cloned.1.call-update) | async-done | bytes 2097168 | tf_op jit(solution)/shard_map/reduce_scatter | solution.py:41
  (10 shorter events, 0.1 us)
Async XLA Ops:
  7.2 95.2 %all-gather.3.cloned.1.call-start = ((), (), s32[]{:S(2)}) async-start(), calls=%async_computation.4 | async-start | bytes 18874368 | tf_op jit(solution)/shard_map/all_gather | solution.py:18
  7.9 244.3 %all-gather.5.cloned.1.call-start = ((), (), s32[]{:S(2)}) async-start(), calls=%async_computation.5 | async-start | bytes 18874368 | tf_op jit(solution)/shard_map/all_gather | solution.py:19
  142.2 99.0 %all-to-all-start = ((f32[16,256,256]{1,2,0:T(8,128)}), f32[16,256,256]{1,2,0:T(8,128)}, u32[]{:S(2)}, u32[]{:S(2)}) async-start(f32[16,256,256]{1,2,0:T(8,128)} %bitcast.46), calls=%async_computation | async-start | bytes 8388608 | tf_op jit(solution)/shard_map/all_to_all | solution.py:25
  147.4 337.7 %reduce-scatter.5.cloned.1.call-start = ((), (), s32[]{:S(2)}) async-start(), calls=%async_computation.7 | async-start | bytes 18874368 | tf_op jit(solution)/shard_map/reduce_scatter | solution.py:31
  252.2 23.3 %copy-start.1 = (f32[4,256,1024]{2,1,0:T(8,128)S(1)}, f32[4,256,1024]{2,1,0:T(8,128)}, u32[]{:S(2)}) copy-start(f32[4,256,1024]{2,1,0:T(8,128)} %all_to_all.27) | copy-start | bytes 12582916
  273.5 2.0 copy-start
  292.2 275.7 %reduce-scatter.3.cloned.1.call-start = ((), (), s32[]{:S(2)}) async-start(), calls=%async_computation.6 | async-start | bytes 18874368 | tf_op jit(solution)/shard_map/reduce_scatter | solution.py:41
  415.5 3.7 copy-start.2
  415.9 21.0 %copy-start.3 = (f32[4,4,256,256]{2,3,1,0:T(8,128)}, f32[4,4,256,256]{2,3,1,0:T(8,128)S(1)}, u32[]{:S(2)}) copy-start(f32[4,4,256,256]{2,3,1,0:T(8,128)S(1)} %copy.51) | copy-start | bytes 12582916
Sparse Core Ops, SparseCore 0:
  9.9 92.4 all-gather.2
  104.3 89.7 all-gather.4
  292.3 114.3 reduce-scatter.4
  453.5 114.4 reduce-scatter.2
where the time goes:
time: 581 us; the launch traced here: 575 us
  waiting for transfers between devices  254 us (44%)
  matrix products  116 us (20%)
  blocking collectives  96.6 us (17%)
  local copies, waits for them, and re-layouts  87.6 us (15%)
  between operations  14.3 us (2%)
    all_to_all x1, blocking collectives, body(): lax.all_to_all(delta_mixed, 'blk', split_axis=2, concat_axis=0, tiled=True)  96.6 us
    all_gather x1, waiting for transfers between devices, body(): lax.all_gather(first_factor, 'tok', axis=1, tiled=True)  87.6 us
    reduce_scatter x1, waiting for transfers between devices, body(): lax.psum_scatter(first_grad, 'tok', scatter_dimension=1, tiled=True)  82.9 us
    all_to_all x1, waiting for transfers between devices, body(): lax.all_to_all(first, 'blk', split_axis=0, concat_axis=2, tiled=True)  82.6 us
    dot_general x1, matrix products, body(): second = jnp.einsum('btk,bko->tbo', mixed, second_whole, precision=hp)  21.3 us
    dot_general x1, matrix products, body(): jnp.einsum('tbi,bisg->stbg', xb, first_view, precision=hp)  20.6 us
    dot_general x1, matrix products, body(): jnp.einsum('tbo,bko->btk', delta_second, second_whole, precision=hp)  20.2 us
    dot_general x1, matrix products, body(): jnp.einsum('stbg,bisg->tbi', delta_view, first_view, precision=hp)  20.1 us
  transfers between devices with their start and end apart: 5, of which 3 were waited for; matrix products, arithmetic and copies ran while one was open for 27% of the time, Pallas kernels for 0%

commit v1 on v0

v1 whole, which is shorter than its diff:
```python
import functools
import math

import jax
import jax.numpy as jnp
from jax import lax
from jax.experimental import pallas as pl
from jax.experimental.pallas import tpu as pltpu
from jax.sharding import PartitionSpec as P


F32 = jnp.float32
BF16 = jnp.bfloat16
LANES = 128


def split(value):
    high = value.astype(BF16)
    return high, (value - high.astype(F32)).astype(BF16)


def product(left, right, dims):
    def one(a, b):
        return lax.dot_general(a, b, (dims, ((), ())), preferred_element_type=F32)

    return one(left[0], right[1]) + one(left[1], right[0]) + one(left[0], right[0])


PLAIN = ((1,), (0,))
TURNED = ((1,), (1,))


def swap_groups(first, second):
    half = LANES // 2
    low = lax.broadcasted_iota(jnp.int32, first.shape, 1) < half
    return (
        jnp.where(low, first, pltpu.roll(second, half, 1)),
        jnp.where(low, pltpu.roll(first, half, 1), second),
    )


def place_rows(pieces, me, high, low):
    for p, piece in enumerate(pieces):
        rows = piece.shape[0]
        at = pl.ds(pl.multiple_of((me ^ p) * rows, rows), rows)
        h, l = split(piece[...])
        high[at, :] = h
        low[at, :] = l


def place_turned(value, first_shard, me, rows, high, low):
    turned = value.T
    h, l = split(turned)
    for u in range(turned.shape[0] // rows):
        at = pl.ds(pl.multiple_of(((first_shard + u) ^ me) * rows, rows), rows)
        high[at, :] = h[u * rows : (u + 1) * rows]
        low[at, :] = l[u * rows : (u + 1) * rows]


def forward_kernel(T, Z, ids, x_ref, *refs):
    pieces = (refs[:T], refs[T : 2 * T])
    outs = refs[2 * T : 2 * T + Z]
    xh, xl, fh, fl = refs[2 * T + Z :]
    me = ids[0]
    step = pl.program_id(0)
    order = x_ref.shape[1] // 2

    @pl.when(step == 0)
    def _():
        h, l = split(x_ref[...])
        xh[...] = h
        xl[...] = l

    results = []
    for i in range(2):
        place_rows(pieces[i], me, fh.at[i], fl.at[i])
        at = slice(i * order, (i + 1) * order)
        results.append(product((xh[:, at], xl[:, at]), (fh[i], fl[i]), PLAIN))
    for c in range(Z):

        @pl.when(step == c)
        def _():
            for h in range(results[0].shape[1] // LANES):
                at = slice(h * LANES, (h + 1) * LANES)
                one, two = swap_groups(results[0][:, at], results[1][:, at])
                outs[c][2 * h] = one
                outs[c][2 * h + 1] = two


def middle_kernel(T, Z, chunks, ids, *refs):
    arrived = refs[: Z * chunks]
    refs = refs[Z * chunks :]
    pieces = (refs[:T], refs[T : 2 * T])
    cots = refs[2 * T : 2 * T + 2]
    odd, even = refs[2 * T + 2 : 2 * T + 4]
    outs = refs[2 * T + 4 : 2 * T + 4 + Z]
    mh, ml, th, tl, sh, sl, back = refs[2 * T + 4 + Z :]
    me, z = ids[0], ids[1]
    rows = pieces[0][0].shape[0]
    step = pl.program_id(0)

    @pl.when(step == 0)
    def _():
        for c in range(Z):
            source = lax.rem(z + (Z - c), Z)
            for k in range(chunks):
                q = source * chunks + k
                for i in range(2):
                    value = arrived[c * chunks + k][i]
                    h, l = split(value)
                    at = pl.ds(pl.multiple_of(q * LANES, LANES), LANES)
                    mh[i, :, at] = h
                    ml[i, :, at] = l
                    place_turned(value, q * (LANES // rows), me, rows, th.at[i], tl.at[i])
        back[...] = jnp.zeros_like(back)

    for i in range(2):
        place_rows(pieces[i], me, sh.at[i], sl.at[i])
        factor = (sh[i], sl[i])
        second = product((mh[i], ml[i]), factor, PLAIN)
        cdf = 0.5 * (1.0 + lax.erf(second * (1.0 / math.sqrt(2.0))))
        density = jnp.exp(-0.5 * second * second) * (1.0 / math.sqrt(2.0 * math.pi))
        delta = split(cots[i][...] * (cdf + second * density))
        grad = product((th[i], tl[i]), delta, PLAIN)
        for p in range(T):
            (odd if p % 2 else even)[i, p // 2] = grad[p * rows : (p + 1) * rows]
        back[i] += product(delta, factor, TURNED)

    @pl.when(step == pl.num_programs(0) - 1)
    def _():
        width = outs[0].shape[0] * LANES // 2
        for c in range(Z):
            start = lax.rem(z + c, Z) * width
            for h in range(width // LANES):
                at = pl.ds(pl.multiple_of(start + h * LANES, LANES), LANES)
                one, two = swap_groups(back[0, :, at], back[1, :, at])
                outs[c][2 * h] = one
                outs[c][2 * h + 1] = two


def backward_kernel(T, Z, chunks, tile, ids, _, x_ref, *refs):
    arrived = refs[: Z * chunks]
    refs = refs[Z * chunks :]
    pieces = (refs[:T], refs[T : 2 * T])
    out, odd, even = refs[2 * T : 2 * T + 3]
    dh, dl, th, tl, fh, fl = refs[2 * T + 3 :]
    me, z = ids[0], ids[1]
    rows = pieces[0][0].shape[0]
    order = x_ref.shape[1] // 2
    step = pl.program_id(0)

    @pl.when(step == 0)
    def _():
        for c in range(Z):
            source = lax.rem(z + (Z - c), Z)
            for k in range(chunks):
                q = source * chunks + k
                at = pl.ds(pl.multiple_of(q * LANES, LANES), LANES)
                for i in range(2):
                    h, l = split(arrived[c * chunks + k][i])
                    dh[i, :, at] = h
                    dl[i, :, at] = l
        for i in range(2):
            for q in range(order // LANES):
                start = i * order + q * LANES
                value = x_ref[:, start : start + LANES]
                place_turned(value, q * (LANES // rows), me, rows, th.at[i], tl.at[i])
        out[...] = jnp.zeros_like(out)

    for i in range(2):
        place_rows(pieces[i], me, fh.at[i], fl.at[i])
        at = pl.ds(pl.multiple_of(step * tile, tile), tile)
        delta = (dh[i, :, at], dl[i, :, at])
        grad = product((th[i], tl[i]), delta, PLAIN)
        for p in range(T):
            (odd if p % 2 else even)[i, p // 2] = grad[p * rows : (p + 1) * rows]
        out[:, i * order : (i + 1) * order] += product(delta, (fh[i], fl[i]), TURNED)


def cost(flops, moved):
    return pl.CostEstimate(flops=flops, bytes_accessed=moved, transcendentals=0)


def params():
    return pltpu.CompilerParams(
        dimension_semantics=("arbitrary",), vmem_limit_bytes=48 * 1024 * 1024
    )


def kernel(*args, **settings):
    return pl.pallas_call(*args, **settings)


def body(inputs, first_factor, second_factor, cotangent):
    T, Z = lax.axis_size("tok"), lax.axis_size("blk")
    LB, rows, order = first_factor.shape
    count = inputs.shape[0]
    group = order // (LB * Z)
    chunks = LB // 2
    width = LB * group
    tile = 256
    steps = order // tile
    half = T // 2
    ids = jnp.stack([lax.axis_index("tok"), lax.axis_index("blk")]).astype(jnp.int32)
    bits = [1 << k for k in range(1, T.bit_length() - 1)]

    def across(value, bit):
        return lax.ppermute(value, "tok", [(d, d ^ bit) for d in range(T)])

    def along(value, c):
        return lax.ppermute(value, "blk", [(d, (d + c) % Z) for d in range(Z)])

    def gather(factor, after=None):
        blocks, last = [], []
        for b in range(LB):
            shard = factor[b]
            if after is not None:
                shard, _ = lax.optimization_barrier((shard, after[0]))
            held = {0: shard}
            for bit in bits if b % 2 == 0 else bits[::-1]:
                held.update({p | bit: across(v, bit) for p, v in list(held.items())})
            last.append(held[T - 2])
            held.update({p | 1: across(v, 1) for p, v in list(held.items())})
            blocks.append([held[p] for p in range(T)])
        return blocks, [(last[2 * k], last[2 * k + 1]) for k in range(chunks)]

    def scatter(odd, even):
        met = across(odd, 1)
        terms = [
            {p: [(even, (i, p // 2)), (met, (i, p // 2))] for p in range(0, T, 2)}
            for i in range(2)
        ]
        sums = None
        for n in range(len(bits)):
            going, sums = [], []
            for i, bit in enumerate((bits[n], bits[::-1][n])):
                going.append([p for p in terms[i] if p & bit])
                sums.append(jnp.stack([total(terms[i].pop(p)) for p in going[i]]))
            sums = lax.optimization_barrier(sums)
            for i, bit in enumerate((bits[n], bits[::-1][n])):
                sent = across(sums[i], bit)
                for m, p in enumerate(going[i]):
                    terms[i][p ^ bit].append((sent, m))
        return [terms[i][0] for i in range(2)], sums

    def total(found):
        return functools.reduce(jnp.add, [array[at] for array, at in found])

    def settle(parts, after):
        arrays = [[[array for array, _ in found] for found in part] for part in parts]
        arrays, _ = lax.optimization_barrier((arrays, after))
        sums = []
        for part, held in zip(parts, arrays):
            for found, group in zip(part, held):
                sums.append(total([(array, at) for array, (_, at) in zip(group, found)]))
        return jnp.stack(sums)

    def full(shape):
        return pl.BlockSpec(shape, lambda n, ids: (0,) * len(shape))

    first_pieces, last = gather(first_factor)
    second_pieces, _ = gather(second_factor, last)

    flops = 2 * 2 * count * order * order
    column = pl.BlockSpec((rows, tile), lambda n, ids: (0, n))

    def exchange(sent):
        arrived = []
        for c in range(Z):
            if c == 0:
                arrived.append([(sent[c], j) for j in range(chunks)])
            elif 2 * c == Z and Z % 4 == 0 and chunks == 2:
                near = along(sent[c][:2], c)
                far = along(sent[c][2:], Z - c // 2)
                far = along(far, Z - c // 2)
                arrived.append([(near, 0), (far, 0)])
            else:
                whole = along(sent[c], c)
                arrived.append([(whole, j) for j in range(chunks)])
        return arrived

    def arrivals(exchanged, j):
        found = [exchanged[k][c][j] for c in range(Z) for k in range(chunks)]
        specs = [
            pl.BlockSpec((2, count, LANES), lambda n, ids, at=at: (at, 0, 0)) for _, at in found
        ]
        return [array for array, _ in found], specs

    mixed = []
    for k in range(chunks):
        sent = kernel(
            functools.partial(forward_kernel, T, Z),
            grid_spec=pltpu.PrefetchScalarGridSpec(
                num_scalar_prefetch=1,
                grid=(Z,),
                in_specs=[pl.BlockSpec((count, 2 * order), lambda n, ids, k=k: (0, k))]
                + [pl.BlockSpec((rows, width), lambda n, ids: (0, lax.rem(ids[1] + n, Z)))]
                * (2 * T),
                out_specs=[full((LB, count, LANES))] * Z,
                scratch_shapes=[pltpu.VMEM((count, 2 * order), BF16)] * 2
                + [pltpu.VMEM((2, order, width), BF16)] * 2,
            ),
            out_shape=[jax.ShapeDtypeStruct((LB, count, LANES), F32)] * Z,
            compiler_params=params(),
            cost_estimate=cost(3 * flops, 4 * 2 * (order * order + 2 * count * order)),
        )(ids, inputs, *first_pieces[2 * k], *first_pieces[2 * k + 1])
        mixed.append(exchange(sent))

    returned = []
    second_parts = []
    for k in range(chunks):
        arrays, specs = arrivals(mixed, k)
        odd, even, *sent = kernel(
            functools.partial(middle_kernel, T, Z, chunks),
            grid_spec=pltpu.PrefetchScalarGridSpec(
                num_scalar_prefetch=1,
                grid=(steps,),
                in_specs=specs
                + [column] * (2 * T)
                + [
                    pl.BlockSpec((count, tile), lambda n, ids, b=b: (0, b * steps + n))
                    for b in (2 * k, 2 * k + 1)
                ],
                out_specs=[pl.BlockSpec((2, half, rows, tile), lambda n, ids: (0, 0, 0, n))] * 2
                + [full((LB, count, LANES))] * Z,
                scratch_shapes=[pltpu.VMEM((2, count, order), BF16)] * 2
                + [pltpu.VMEM((2, order, count), BF16)] * 2
                + [pltpu.VMEM((2, order, tile), BF16)] * 2
                + [pltpu.VMEM((2, count, order), F32)],
            ),
            out_shape=[jax.ShapeDtypeStruct((2, half, rows, order), F32)] * 2
            + [jax.ShapeDtypeStruct((LB, count, LANES), F32)] * Z,
            compiler_params=params(),
            cost_estimate=cost(9 * flops, 4 * 2 * (2 * order * order + 3 * count * order)),
        )(
            ids,
            *arrays,
            *second_pieces[2 * k],
            *second_pieces[2 * k + 1],
            cotangent,
            cotangent,
        )
        returned.append(exchange(sent))
        second_parts.append(scatter(odd, even)[0])

    first_parts = []
    input_grad = None
    for k in range(chunks):
        arrays, specs = arrivals(returned, k)
        args = (inputs, *arrays, *first_pieces[2 * k], *first_pieces[2 * k + 1])
        before = ids if input_grad is None else input_grad
        input_grad, odd, even = kernel(
            functools.partial(backward_kernel, T, Z, chunks, tile),
            grid_spec=pltpu.PrefetchScalarGridSpec(
                num_scalar_prefetch=1,
                grid=(steps,),
                in_specs=[pl.BlockSpec(memory_space=pl.ANY)]
                + [pl.BlockSpec((count, 2 * order), lambda n, ids, k=k: (0, k))]
                + specs
                + [column] * (2 * T),
                out_specs=[pl.BlockSpec((count, 2 * order), lambda n, ids, k=k: (0, k))]
                + [pl.BlockSpec((2, half, rows, tile), lambda n, ids: (0, 0, 0, n))] * 2,
                scratch_shapes=[pltpu.VMEM((2, count, order), BF16)] * 2
                + [pltpu.VMEM((2, order, count), BF16)] * 2
                + [pltpu.VMEM((2, order, tile), BF16)] * 2,
            ),
            out_shape=[jax.ShapeDtypeStruct(inputs.shape, F32)]
            + [jax.ShapeDtypeStruct((2, half, rows, order), F32)] * 2,
            compiler_params=params(),
            cost_estimate=cost(6 * flops, 4 * 2 * (2 * order * order + 3 * count * order)),
            input_output_aliases={} if k == 0 else {1: 0},
        )(ids, before, *args)
        part, last = scatter(odd, even)
        first_parts.append(part)
    second_out = settle(second_parts, input_grad)
    return (input_grad, settle(first_parts, last), second_out)


def solution(mesh):
    placed = (P("tok", "blk"), P("blk", "tok", None), P("blk", "tok", None), P("tok", "blk"))

    return jax.shard_map(
        body,
        mesh=mesh,
        in_specs=placed,
        out_specs=(P("tok", "blk"), P("blk", "tok", None), P("blk", "tok", None)),
        check_vma=False,
    )
```

time: 581 us -> 545 us (0.938)
  matrix products: 116 us -> 0 us
  starting transfers between devices: 5.5 us -> 109 us
  blocking collectives: 96.6 us -> 0 us
  Pallas kernels: 0 us -> 92.6 us
  local copies, waits for them, and re-layouts: 87.6 us -> 12.2 us
  waiting for transfers between devices: 254 us -> 311 us
  other arithmetic: 0 us -> 18.3 us
  between operations: 14.3 us -> 1.39 us
    ppermute x0 -> x96, waiting for transfers between devices: none -> 311 us  [the longest x76 215 us: across(): return lax.ppermute(value, 'tok', [(d, d ^ bit) for d in range(T)])]
    dot_general x6 -> x0, matrix products: 116 us -> none  [the longest x1 21.3 us: body(): second = jnp.einsum('btk,bko->tbo', mixed, second_whole, precision=hp)]
    ppermute x0 -> x96, starting transfers between devices: none -> 109 us  [the longest x20 59.2 us: along(): return lax.ppermute(value, 'blk', [(d, (d + c) % Z) for d in range(Z)])]
    all_to_all x1 -> x0, blocking collectives: 96.6 us -> none  [body(): lax.all_to_all(delta_mixed, 'blk', split_axis=2, concat_axis=0, tiled=True)]
    pallas_call x0 -> x6, Pallas kernels: none -> 92.6 us  [the longest x2 42.4 us: body(): kernel(functools.partial(middle_kernel, T, Z, chunks), grid_spec=pltpu.Pr...]
    all_gather x2 -> x0, waiting for transfers between devices: 87.6 us -> none  [the longest x1 87.6 us: body(): lax.all_gather(first_factor, 'tok', axis=1, tiled=True)]
    reduce_scatter x2 -> x0, waiting for transfers between devices: 82.9 us -> none  [the longest x1 82.9 us: body(): lax.psum_scatter(first_grad, 'tok', scatter_dimension=1, tiled=True)]
    all_to_all x1 -> x0, waiting for transfers between devices: 82.6 us -> none  [body(): lax.all_to_all(first, 'blk', split_axis=0, concat_axis=2, tiled=True)]
  transfers between devices with their start and end apart: 5 -> 96, of which waited for: 3 -> 32; matrix products, arithmetic and copies ran while one was open for 27% -> 3% of each run, Pallas kernels for 0% -> 17%
where the time goes in v1:
time: 545 us; the launch traced here: 544 us
  waiting for transfers between devices  311 us (57%)
  starting transfers between devices  109 us (20%)
  Pallas kernels  92.6 us (17%)
  other arithmetic  18.3 us (3%)
  local copies, waits for them, and re-layouts  12.2 us (2%)
    ppermute x76, waiting for transfers between devices, across(): return lax.ppermute(value, 'tok', [(d, d ^ bit) for d in range(T)])  215 us
    ppermute x20, waiting for transfers between devices, along(): return lax.ppermute(value, 'blk', [(d, (d + c) % Z) for d in range(Z)])  96.5 us
    ppermute x20, starting transfers between devices, along(): return lax.ppermute(value, 'blk', [(d, (d + c) % Z) for d in range(Z)])  59.2 us
    ppermute x76, starting transfers between devices, across(): return lax.ppermute(value, 'tok', [(d, d ^ bit) for d in range(T)])  49.4 us
    pallas_call x2, Pallas kernels, body(): kernel(functools.partial(middle_kernel, T, Z, chunks), grid_spec=pltpu.Pr...  42.4 us
    pallas_call x2, Pallas kernels, body(): kernel(functools.partial(backward_kernel, T, Z, chunks, tile), grid_spec=...  29.4 us
    pallas_call x2, Pallas kernels, body(): kernel(functools.partial(forward_kernel, T, Z), grid_spec=pltpu.PrefetchS...  20.8 us
    add x16, other arithmetic, total(): return functools.reduce(jnp.add, [array[at] for array, at in found])  14.2 us
  transfers between devices with their start and end apart: 96, of which 32 were waited for; matrix products, arithmetic and copies ran while one was open for 3% of the time, Pallas kernels for 17%

profile of v1, /device:TPU:0, one launch (start us, length us, event | category | flops | bytes accessed | tf_op | source)
XLA Modules:
  0.0 544.2 jit_solution(9161557028792409876)
XLA Ops:
  7.7 10.7 %collective-permute-done.24.refs_12_.refs_20_ = f32[128,1024]{1,0:T(8,128)S(1)} collective-permute-done((f32[128,1024]{1,0:T(8,128)S(1)}, f32[128,1024]{1,0:T(8,128)S(1)}, u32[]{:S(2)}, u32[]{:S(2)}) %collective-permute-start.24) | collective-permute-done | bytes 524320 | tf_op jit(solution)/shard_map/ppermute | solution.py:208
  22.4 7.2 %collective-permute-done.10.refs_12_.refs_20_ = f32[128,1024]{1,0:T(8,128)S(1)} collective-permute-done((f32[128,1024]{1,0:T(8,128)S(1)}, f32[128,1024]{1,0:T(8,128)S(1)}, u32[]{:S(2)}, u32[]{:S(2)}) %collective-permute-start.10) | collective-permute-done | bytes 524320 | tf_op jit(solution)/shard_map/ppermute | solution.py:208
  33.7 7.1 %collective-permute-done.3.refs_4_.refs_12_ = f32[128,1024]{1,0:T(8,128)S(1)} collective-permute-done((f32[128,1024]{1,0:T(8,128)S(1)}, f32[128,1024]{1,0:T(8,128)S(1)}, u32[]{:S(2)}, u32[]{:S(2)}) %collective-permute-start.3) | collective-permute-done | bytes 524320 | tf_op jit(solution)/shard_map/ppermute | solution.py:208
  45.2 6.1 %collective-permute-done.17.refs_4_.refs_12_ = f32[128,1024]{1,0:T(8,128)S(1)} collective-permute-done((f32[128,1024]{1,0:T(8,128)S(1)}, f32[128,1024]{1,0:T(8,128)S(1)}, u32[]{:S(2)}, u32[]{:S(2)}) %collective-permute-start.17) | collective-permute-done | bytes 524320 | tf_op jit(solution)/shard_map/ppermute | solution.py:208
  55.6 9.7 %collective-permute-done.26.refs_14_.refs_22_ = f32[128,1024]{1,0:T(8,128)S(1)} collective-permute-done((f32[128,1024]{1,0:T(8,128)S(1)}, f32[128,1024]{1,0:T(8,128)S(1)}, u32[]{:S(2)}, u32[]{:S(2)}) %collective-permute-start.26) | collective-permute-done | bytes 524320 | tf_op jit(solution)/shard_map/ppermute | solution.py:208
  66.0 9.2 %collective-permute-done.12.refs_14_.refs_22_ = f32[128,1024]{1,0:T(8,128)S(1)} collective-permute-done((f32[128,1024]{1,0:T(8,128)S(1)}, f32[128,1024]{1,0:T(8,128)S(1)}, u32[]{:S(2)}, u32[]{:S(2)}) %collective-permute-start.12) | collective-permute-done | bytes 524320 | tf_op jit(solution)/shard_map/ppermute | solution.py:208
  84.9 6.3 %collective-permute-done.19.refs_6_.refs_14_ = f32[128,1024]{1,0:T(8,128)} collective-permute-done((f32[128,1024]{1,0:T(8,128)S(1)}, f32[128,1024]{1,0:T(8,128)}, u32[]{:S(2)}, u32[]{:S(2)}) %collective-permute-start.19) | collective-permute-done | bytes 524320 | tf_op jit(solution)/shard_map/ppermute | solution.py:208
  96.4 10.8 %collective-permute-done.55.refs_12_ = f32[128,1024]{1,0:T(8,128)} collective-permute-done((f32[128,1024]{1,0:T(8,128)}, f32[128,1024]{1,0:T(8,128)}, u32[]{:S(2)}, u32[]{:S(2)}) %collective-permute-start.55) | collective-permute-done | bytes 524320 | tf_op jit(solution)/shard_map/ppermute | solution.py:208
  109.3 10.4 %shard_map.68 = (f32[4,256,128]{2,1,0:T(8,128)S(1)}, f32[4,256,128]{2,1,0:T(8,128)S(1)}, f32[4,256,128]{2,1,0:T(8,128)S(1)}, f32[4,256,128]{2,1,0:T(8,128)S(1)}) custom-call(s32[2]{0:T(128)S(1)} %pad_add_fusion.ids._, f32[256,4096]{1,0:T(8,128)} %x_ref.7, f32[128,1024]{1,0:T(8,128)S(1)} %get-tuple-element.190.refs_0_.refs_8_, ...), custom_call_target="tpu_custom_call" | custom-call | flops 3221225472 | bytes 12582912 | tf_op jit(solution)/shard_map/pallas_call | solution.py:291
  121.8 10.4 %shard_map.67 = (f32[4,256,128]{2,1,0:T(8,128)S(1)}, f32[4,256,128]{2,1,0:T(8,128)S(1)}, f32[4,256,128]{2,1,0:T(8,128)S(1)}, f32[4,256,128]{2,1,0:T(8,128)S(1)}) custom-call(s32[2]{0:T(128)S(1)} %pad_add_fusion.ids._, f32[256,4096]{1,0:T(8,128)} %x_ref.7, f32[128,1024]{1,0:T(8,128)S(1)} %get-tuple-element.189.refs_0_.refs_8_, f32[128,1024]{1,0:T(8,128)S(1)} %copy-done.5, ...), custom_call_target="tpu_custom_call" | custom-call | flops 3221225472 | bytes 12582912 | tf_op jit(solution)/shard_map/pallas_call | solution.py:291
  138.7 7.9 %collective-permute-done.62.refs_20_ = f32[128,1024]{1,0:T(8,128)S(1)} collective-permute-done((f32[128,1024]{1,0:T(8,128)S(1)}, f32[128,1024]{1,0:T(8,128)S(1)}, u32[]{:S(2)}, u32[]{:S(2)}) %collective-permute-start.62) | collective-permute-done | bytes 524320 | tf_op jit(solution)/shard_map/ppermute | solution.py:208
  155.2 12.7 %collective-permute-done.31.refs_5_ = f32[2,256,128]{2,1,0:T(8,128)S(1)} collective-permute-done((f32[2,256,128]{2,1,0:T(8,128)S(1)}, f32[2,256,128]{2,1,0:T(8,128)S(1)}, u32[]{:S(2)}, u32[]{:S(2)}) %collective-permute-start.31) | collective-permute-done | bytes 262176 | tf_op jit(solution)/shard_map/ppermute | solution.py:211
  167.9 14.8 %collective-permute-start.33 = (f32[4,256,128]{2,1,0:T(8,128)S(1)}, f32[4,256,128]{2,1,0:T(8,128)S(1)}, u32[]{:S(2)}, u32[]{:S(2)}) collective-permute-start(f32[4,256,128]{2,1,0:T(8,128)S(1)} %get-tuple-element.88), channel_id=1, source_target_pairs={{0,24},{8,0},{16,8},{24,16},{1,25},{9,1},{17,9},{25,17},{2,26},{10... | collective-permute-start | bytes 1572872 | tf_op jit(solution)/shard_map/ppermute | solution.py:211
  190.0 7.2 %collective-permute-done.33.refs_7_ = f32[4,256,128]{2,1,0:T(8,128)S(1)} collective-permute-done((f32[4,256,128]{2,1,0:T(8,128)S(1)}, f32[4,256,128]{2,1,0:T(8,128)S(1)}, u32[]{:S(2)}, u32[]{:S(2)}) %collective-permute-start.33) | collective-permute-done | bytes 524320 | tf_op jit(solution)/shard_map/ppermute | solution.py:211
  197.3 11.1 %collective-permute-done.28.refs_2_ = f32[4,256,128]{2,1,0:T(8,128)S(1)} collective-permute-done((f32[4,256,128]{2,1,0:T(8,128)S(1)}, f32[4,256,128]{2,1,0:T(8,128)S(1)}, u32[]{:S(2)}, u32[]{:S(2)}) %collective-permute-start.28) | collective-permute-done | bytes 524320 | tf_op jit(solution)/shard_map/ppermute | solution.py:211
  208.4 10.1 %collective-permute-done.32.refs_6_ = f32[4,256,128]{2,1,0:T(8,128)S(1)} collective-permute-done((f32[4,256,128]{2,1,0:T(8,128)S(1)}, f32[4,256,128]{2,1,0:T(8,128)S(1)}, u32[]{:S(2)}, u32[]{:S(2)}) %collective-permute-start.32) | collective-permute-done | bytes 524320 | tf_op jit(solution)/shard_map/ppermute | solution.py:211
  222.4 10.1 %collective-permute-done.39.refs_14_ = f32[128,1024]{1,0:T(8,128)S(1)} collective-permute-done((f32[128,1024]{1,0:T(8,128)S(1)}, f32[128,1024]{1,0:T(8,128)S(1)}, u32[]{:S(2)}, u32[]{:S(2)}) %collective-permute-start.39) | collective-permute-done | bytes 524320 | tf_op jit(solution)/shard_map/ppermute | solution.py:208
  234.6 10.1 %collective-permute-done.46.refs_22_ = f32[128,1024]{1,0:T(8,128)S(1)} collective-permute-done((f32[128,1024]{1,0:T(8,128)S(1)}, f32[128,1024]{1,0:T(8,128)S(1)}, u32[]{:S(2)}, u32[]{:S(2)}) %collective-permute-start.46) | collective-permute-done | bytes 524320 | tf_op jit(solution)/shard_map/ppermute | solution.py:208
  246.6 21.3 %shard_map.70 = (f32[2,4,128,1024]{3,2,1,0:T(8,128)}, f32[2,4,128,1024]{3,2,1,0:T(8,128)}, f32[4,256,128]{2,1,0:T(8,128)S(1)}, f32[4,256,128]{2,1,0:T(8,128)S(1)...) custom-call(s32[2]{0:T(128)S(1)} %pad_add_fusion.ids._, f32[4,256,128]{2,1,0:T(8,128)S(1)} %get-tuple-element.81.refs_0_, ...), custom_call_target="tpu_custom_call" | custom-call | flops 9663676416 | bytes 23068672 | tf_op jit(solution)/shard_map/pallas_call | solution.py:313
  272.9 8.4 %collective-permute-start.69 = (f32[2,256,128]{2,1,0:T(8,128)S(1)}, f32[2,256,128]{2,1,0:T(8,128)S(1)}, u32[]{:S(2)}, u32[]{:S(2)}) collective-permute-start(f32[2,256,128]{2,1,0:T(8,128)S(1)} %get-tuple-element.192), channel_id=1, source_target_pairs={{0,16},{8,24},{16,0},{24,8},{1,17},{9,25},{17,1},{25,9},{2,18},{10... | collective-permute-start | bytes 786440 | tf_op jit(solution)/shard_map/ppermute | solution.py:211
  281.4 21.2 %shard_map.69 = (f32[2,4,128,1024]{3,2,1,0:T(8,128)}, f32[2,4,128,1024]{3,2,1,0:T(8,128)}, f32[4,256,128]{2,1,0:T(8,128)S(1)}, f32[4,256,128]{2,1,0:T(8,128)S(1)...) custom-call(s32[2]{0:T(128)S(1)} %pad_add_fusion.ids._, f32[4,256,128]{2,1,0:T(8,128)S(1)} %get-tuple-element.81.refs_0_, ...), custom_call_target="tpu_custom_call" | custom-call | flops 9663676416 | bytes 23068672 | tf_op jit(solution)/shard_map/pallas_call | solution.py:313
  311.7 11.4 %collective-permute-done.72 = f32[2,256,128]{2,1,0:T(8,128)S(1)} collective-permute-done((f32[2,256,128]{2,1,0:T(8,128)S(1)}, f32[2,256,128]{2,1,0:T(8,128)S(1)}, u32[]{:S(2)}, u32[]{:S(2)}) %collective-permute-start.72) | collective-permute-done | bytes 262176 | tf_op jit(solution)/shard_map/ppermute | solution.py:211
  324.0 44.0 %collective-permute-done.68.refs_4_ = f32[2,256,128]{2,1,0:T(8,128)S(1)} collective-permute-done((f32[2,256,128]{2,1,0:T(8,128)S(1)}, f32[2,256,128]{2,1,0:T(8,128)S(1)}, u32[]{:S(2)}, u32[]{:S(2)}) %collective-permute-start.68) | collective-permute-done | bytes 262176 | tf_op jit(solution)/shard_map/ppermute | solution.py:211
  370.9 14.5 %shard_map.71 = (f32[256,4096]{1,0:T(8,128)}, f32[2,4,128,1024]{3,2,1,0:T(8,128)}, f32[2,4,128,1024]{3,2,1,0:T(8,128)}) custom-call(s32[2]{0:T(128)S(1)} %pad_add_fusion.ids._, s32[2]{0:T(128)S(1)} %pad_add_fusion.ids._, f32[256,4096]{1,0:T(8,128)} %x_ref.7, f32[4,256,128]{2,1,0:T(8,128)S(1)} %get-tuple-element.91.refs_0_, ...), custom_call_target="tpu_custom_call" | custom-call | flops 6442450944 | bytes 23068672 | tf_op jit(solution)/shard_map/pallas_call | solution.py:352
  385.5 14.9 %shard_map.72 = (f32[256,4096]{1,0:T(8,128)}, f32[2,4,128,1024]{3,2,1,0:T(8,128)}, f32[2,4,128,1024]{3,2,1,0:T(8,128)}) custom-call(s32[2]{0:T(128)S(1)} %pad_add_fusion.ids._, f32[256,4096]{1,0:T(8,128)} %get-tuple-element.101._, f32[256,4096]{1,0:T(8,128)} %x_ref.7, f32[4,256,128]{2,1,0:T(8,128)S(1)} %get-tuple-element.91.refs_0_, ...), custom_call_target="tpu_custom_call", output_to_operand_aliasing={{0}: (1, {})} | custom-call | flops 6442450944 | bytes 23068672 | tf_op jit(solution)/shard_map/pallas_call | solution.py:352
  416.0 13.4 %collective-permute-done.92 = f32[2,128,1024]{2,1,0:T(8,128)S(1)} collective-permute-done((f32[2,128,1024]{2,1,0:T(8,128)S(1)}, f32[2,128,1024]{2,1,0:T(8,128)S(1)}, u32[]{:S(2)}, u32[]{:S(2)}) %collective-permute-start.92) | collective-permute-done | bytes 1048608 | tf_op jit(solution)/shard_map/ppermute | solution.py:208
  432.4 19.5 %collective-permute-done.87 = f32[2,128,1024]{2,1,0:T(8,128)S(1)} collective-permute-done((f32[2,128,1024]{2,1,0:T(8,128)S(1)}, f32[2,128,1024]{2,1,0:T(8,128)S(1)}, u32[]{:S(2)}, u32[]{:S(2)}) %collective-permute-start.87) | collective-permute-done | bytes 1048608 | tf_op jit(solution)/shard_map/ppermute | solution.py:208
  456.9 17.4 %collective-permute-done.82 = f32[2,128,1024]{2,1,0:T(8,128)S(1)} collective-permute-done((f32[2,128,1024]{2,1,0:T(8,128)S(1)}, f32[2,128,1024]{2,1,0:T(8,128)S(1)}, u32[]{:S(2)}, u32[]{:S(2)}) %collective-permute-start.82) | collective-permute-done | bytes 1048608 | tf_op jit(solution)/shard_map/ppermute | solution.py:208
  477.3 19.5 %collective-permute-done.77 = f32[2,128,1024]{2,1,0:T(8,128)S(1)} collective-permute-done((f32[2,128,1024]{2,1,0:T(8,128)S(1)}, f32[2,128,1024]{2,1,0:T(8,128)S(1)}, u32[]{:S(2)}, u32[]{:S(2)}) %collective-permute-start.77) | collective-permute-done | bytes 1048608 | tf_op jit(solution)/shard_map/ppermute | solution.py:208
  500.5 9.0 %collective-permute-done.94 = f32[1,128,1024]{2,1,0:T(8,128)S(1)} collective-permute-done((f32[1,128,1024]{2,1,0:T(8,128)S(1)}, f32[1,128,1024]{2,1,0:T(8,128)S(1)}, u32[]{:S(2)}, u32[]{:S(2)}) %collective-permute-start.94) | collective-permute-done | bytes 524320 | tf_op jit(solution)/shard_map/ppermute | solution.py:208
  511.6 9.2 %collective-permute-done.89 = f32[1,128,1024]{2,1,0:T(8,128)S(1)} collective-permute-done((f32[1,128,1024]{2,1,0:T(8,128)S(1)}, f32[1,128,1024]{2,1,0:T(8,128)S(1)}, u32[]{:S(2)}, u32[]{:S(2)}) %collective-permute-start.89) | collective-permute-done | bytes 524320 | tf_op jit(solution)/shard_map/ppermute | solution.py:208
  532.0 10.1 %collective-permute-done.79 = f32[1,128,1024]{2,1,0:T(8,128)S(1)} collective-permute-done((f32[1,128,1024]{2,1,0:T(8,128)S(1)}, f32[1,128,1024]{2,1,0:T(8,128)S(1)}, u32[]{:S(2)}, u32[]{:S(2)}) %collective-permute-start.79) | collective-permute-done | bytes 524320 | tf_op jit(solution)/shard_map/ppermute | solution.py:208
  (315 shorter events, 137.5 us)
Async XLA Ops:
  95.8 36.4 %collective-permute-start.35 = (f32[128,1024]{1,0:T(8,128)}, f32[128,1024]{1,0:T(8,128)S(1)}, u32[]{:S(2)}, u32[]{:S(2)}) collective-permute-start(f32[128,1024]{1,0:T(8,128)} %get-tuple-element.89.refs_8_), channel_id=1, source_target_pairs={{0,2},{1,3},{2,0},{3,1},{4,6},{5,7},{6,4},{7,5},{8,10},{9,11},{10,... | collective-permute-start | bytes 1572872 | tf_op jit(solution)/shard_map/ppermute | solution.py:208
  149.2 33.4 %collective-permute-start.30 = (f32[2,256,128]{2,1,0:T(8,128)S(1)}, f32[2,256,128]{2,1,0:T(8,128)S(1)}, u32[]{:S(2)}, u32[]{:S(2)}) collective-permute-start(f32[2,256,128]{2,1,0:T(8,128)S(1)} %get-tuple-element.198), channel_id=1, source_target_pairs={{0,16},{8,24},{16,0},{24,8},{1,17},{9,25},{17,1},{25,9},{2,18},{10... | collective-permute-start | bytes 786440 | tf_op jit(solution)/shard_map/ppermute | solution.py:211
  150.5 35.1 %collective-permute-start.51 = (f32[2,256,128]{2,1,0:T(8,128)S(1)}, f32[2,256,128]{2,1,0:T(8,128)S(1)}, u32[]{:S(2)}, u32[]{:S(2)}) collective-permute-start(f32[2,256,128]{2,1,0:T(8,128)S(1)} %collective-permute-done.50), channel_id=1, source_target_pairs={{0,24},{8,0},{16,8},{24,16},{1,25},{9,1},{17,9},{25,17},{2,26},{10... | collective-permute-start | bytes 786440 | tf_op jit(solution)/shard_map/ppermute | solution.py:211
  153.2 35.5 %collective-permute-start.49 = (f32[2,256,128]{2,1,0:T(8,128)S(1)}, f32[2,256,128]{2,1,0:T(8,128)S(1)}, u32[]{:S(2)}, u32[]{:S(2)}) collective-permute-start(f32[2,256,128]{2,1,0:T(8,128)S(1)} %collective-permute-done.48), channel_id=1, source_target_pairs={{0,24},{8,0},{16,8},{24,16},{1,25},{9,1},{17,9},{25,17},{2,26},{10... | collective-permute-start | bytes 786440 | tf_op jit(solution)/shard_map/ppermute | solution.py:211
  154.9 33.8 %collective-permute-start.29 = (f32[4,256,128]{2,1,0:T(8,128)S(1)}, f32[4,256,128]{2,1,0:T(8,128)S(1)}, u32[]{:S(2)}, u32[]{:S(2)}) collective-permute-start(f32[4,256,128]{2,1,0:T(8,128)S(1)} %get-tuple-element.84), channel_id=1, source_target_pairs={{0,8},{8,16},{16,24},{24,0},{1,9},{9,17},{17,25},{25,1},{2,10},{10... | collective-permute-start | bytes 1572872 | tf_op jit(solution)/shard_map/ppermute | solution.py:211
  167.9 29.3 %collective-permute-start.33 = (f32[4,256,128]{2,1,0:T(8,128)S(1)}, f32[4,256,128]{2,1,0:T(8,128)S(1)}, u32[]{:S(2)}, u32[]{:S(2)}) collective-permute-start(f32[4,256,128]{2,1,0:T(8,128)S(1)} %get-tuple-element.88), channel_id=1, source_target_pairs={{0,24},{8,0},{16,8},{24,16},{1,25},{9,1},{17,9},{25,17},{2,26},{10... | collective-permute-start | bytes 1572872 | tf_op jit(solution)/shard_map/ppermute | solution.py:211
  185.6 33.0 %collective-permute-start.32 = (f32[4,256,128]{2,1,0:T(8,128)S(1)}, f32[4,256,128]{2,1,0:T(8,128)S(1)}, u32[]{:S(2)}, u32[]{:S(2)}) collective-permute-start(f32[4,256,128]{2,1,0:T(8,128)S(1)} %get-tuple-element.87), channel_id=1, source_target_pairs={{0,24},{8,0},{16,8},{24,16},{1,25},{9,1},{17,9},{25,17},{2,26},{10... | collective-permute-start | bytes 1572872 | tf_op jit(solution)/shard_map/ppermute | solution.py:211
  188.7 31.1 %collective-permute-start.56 = (f32[128,1024]{1,0:T(8,128)}, f32[128,1024]{1,0:T(8,128)S(1)}, u32[]{:S(2)}, u32[]{:S(2)}) collective-permute-start(f32[128,1024]{1,0:T(8,128)} %collective-permute-done.55.refs_12_), channel_id=1, source_target_pairs={{0,1},{1,0},{2,3},{3,2},{4,5},{5,4},{6,7},{7,6},{8,9},{9,8},{10,11... | collective-permute-start | bytes 1572872 | tf_op jit(solution)/shard_map/ppermute | solution.py:208
  188.7 31.8 %collective-permute-start.57 = (f32[128,1024]{1,0:T(8,128)}, f32[128,1024]{1,0:T(8,128)S(1)}, u32[]{:S(2)}, u32[]{:S(2)}) collective-permute-start(f32[128,1024]{1,0:T(8,128)} %collective-permute-done.53.refs_10_), channel_id=1, source_target_pairs={{0,4},{1,5},{2,6},{3,7},{4,0},{5,1},{6,2},{7,3},{8,12},{9,13},{10,... | collective-permute-start | bytes 1572872 | tf_op jit(solution)/shard_map/ppermute | solution.py:208
  245.3 36.1 %collective-permute-start.43 = (f32[128,1024]{1,0:T(8,128)S(1)}, f32[128,1024]{1,0:T(8,128)}, u32[]{:S(2)}, u32[]{:S(2)}) collective-permute-start(f32[128,1024]{1,0:T(8,128)S(1)} %collective-permute-done.42.refs_18_), channel_id=1, source_target_pairs={{0,1},{1,0},{2,3},{3,2},{4,5},{5,4},{6,7},{7,6},{8,9},{9,8},{10,11... | collective-permute-start | bytes 1572872 | tf_op jit(solution)/shard_map/ppermute | solution.py:208
  245.3 36.0 %collective-permute-start.40 = (f32[128,1024]{1,0:T(8,128)S(1)}, f32[128,1024]{1,0:T(8,128)}, u32[]{:S(2)}, u32[]{:S(2)}) collective-permute-start(f32[128,1024]{1,0:T(8,128)S(1)} %collective-permute-done.39.refs_14_), channel_id=1, source_target_pairs={{0,1},{1,0},{2,3},{3,2},{4,5},{5,4},{6,7},{7,6},{8,9},{9,8},{10,11... | collective-permute-start | bytes 1572872 | tf_op jit(solution)/shard_map/ppermute | solution.py:208
  245.8 35.6 %collective-permute-start.47 = (f32[128,1024]{1,0:T(8,128)S(1)}, f32[128,1024]{1,0:T(8,128)}, u32[]{:S(2)}, u32[]{:S(2)}) collective-permute-start(f32[128,1024]{1,0:T(8,128)S(1)} %collective-permute-done.46.refs_22_), channel_id=1, source_target_pairs={{0,1},{1,0},{2,3},{3,2},{4,5},{5,4},{6,7},{7,6},{8,9},{9,8},{10,11... | collective-permute-start | bytes 1572872 | tf_op jit(solution)/shard_map/ppermute | solution.py:208
  268.0 39.9 %collective-permute-start.74 = (f32[2,256,128]{2,1,0:T(8,128)S(1)}, f32[2,256,128]{2,1,0:T(8,128)S(1)}, u32[]{:S(2)}, u32[]{:S(2)}) collective-permute-start(f32[2,256,128]{2,1,0:T(8,128)S(1)} %get-tuple-element.191), channel_id=1, source_target_pairs={{0,24},{8,0},{16,8},{24,16},{1,25},{9,1},{17,9},{25,17},{2,26},{10... | collective-permute-start | bytes 786440 | tf_op jit(solution)/shard_map/ppermute | solution.py:211
  272.9 34.9 %collective-permute-start.69 = (f32[2,256,128]{2,1,0:T(8,128)S(1)}, f32[2,256,128]{2,1,0:T(8,128)S(1)}, u32[]{:S(2)}, u32[]{:S(2)}) collective-permute-start(f32[2,256,128]{2,1,0:T(8,128)S(1)} %get-tuple-element.192), channel_id=1, source_target_pairs={{0,16},{8,24},{16,0},{24,8},{1,17},{9,25},{17,1},{25,9},{2,18},{10... | collective-permute-start | bytes 786440 | tf_op jit(solution)/shard_map/ppermute | solution.py:211
  304.0 64.0 %collective-permute-start.67 = (f32[4,256,128]{2,1,0:T(8,128)S(1)}, f32[4,256,128]{2,1,0:T(8,128)S(1)}, u32[]{:S(2)}, u32[]{:S(2)}) collective-permute-start(f32[4,256,128]{2,1,0:T(8,128)S(1)} %get-tuple-element.96), channel_id=1, source_target_pairs={{0,8},{8,16},{16,24},{24,0},{1,9},{9,17},{17,25},{25,1},{2,10},{10... | collective-permute-start | bytes 1572872 | tf_op jit(solution)/shard_map/ppermute | solution.py:211
  304.7 63.9 %collective-permute-start.71 = (f32[4,256,128]{2,1,0:T(8,128)S(1)}, f32[4,256,128]{2,1,0:T(8,128)S(1)}, u32[]{:S(2)}, u32[]{:S(2)}) collective-permute-start(f32[4,256,128]{2,1,0:T(8,128)S(1)} %get-tuple-element.100), channel_id=1, source_target_pairs={{0,24},{8,0},{16,8},{24,16},{1,25},{9,1},{17,9},{25,17},{2,26},{10... | collective-permute-start | bytes 1572872 | tf_op jit(solution)/shard_map/ppermute | solution.py:211
  307.9 62.8 %collective-permute-start.66 = (f32[4,256,128]{2,1,0:T(8,128)S(1)}, f32[4,256,128]{2,1,0:T(8,128)S(1)}, u32[]{:S(2)}, u32[]{:S(2)}) collective-permute-start(f32[4,256,128]{2,1,0:T(8,128)S(1)} %get-tuple-element.95), channel_id=1, source_target_pairs={{0,8},{8,16},{16,24},{24,0},{1,9},{9,17},{17,25},{25,1},{2,10},{10... | collective-permute-start | bytes 1572872 | tf_op jit(solution)/shard_map/ppermute | solution.py:211
  307.9 63.1 %collective-permute-start.70 = (f32[4,256,128]{2,1,0:T(8,128)S(1)}, f32[4,256,128]{2,1,0:T(8,128)S(1)}, u32[]{:S(2)}, u32[]{:S(2)}) collective-permute-start(f32[4,256,128]{2,1,0:T(8,128)S(1)} %get-tuple-element.99), channel_id=1, source_target_pairs={{0,24},{8,0},{16,8},{24,16},{1,25},{9,1},{17,9},{25,17},{2,26},{10... | collective-permute-start | bytes 1572872 | tf_op jit(solution)/shard_map/ppermute | solution.py:211
  323.1 45.0 %collective-permute-start.68 = (f32[2,256,128]{2,1,0:T(8,128)S(1)}, f32[2,256,128]{2,1,0:T(8,128)S(1)}, u32[]{:S(2)}, u32[]{:S(2)}) collective-permute-start(f32[2,256,128]{2,1,0:T(8,128)S(1)} %get-tuple-element.194), channel_id=1, source_target_pairs={{0,16},{8,24},{16,0},{24,8},{1,17},{9,25},{17,1},{25,9},{2,18},{10... | collective-permute-start | bytes 786440 | tf_op jit(solution)/shard_map/ppermute | solution.py:211
  368.0 32.9 %collective-permute-start.91 = (f32[2,4,128,1024]{3,2,1,0:T(8,128)}, f32[2,4,128,1024]{3,2,1,0:T(8,128)}, u32[]{:S(2)}, u32[]{:S(2)}) collective-permute-start(f32[2,4,128,1024]{3,2,1,0:T(8,128)} %get-tuple-element.138), channel_id=1, source_target_pairs={{0,1},{1,0},{2,3},{3,2},{4,5},{5,4},{6,7},{7,6},{8,9},{9,8},{10,11... | collective-permute-start | bytes 12582920 | tf_op jit(solution)/shard_map/ppermute | solution.py:208
  368.0 38.3 %collective-permute-start.86 = (f32[2,4,128,1024]{3,2,1,0:T(8,128)}, f32[2,4,128,1024]{3,2,1,0:T(8,128)}, u32[]{:S(2)}, u32[]{:S(2)}) collective-permute-start(f32[2,4,128,1024]{3,2,1,0:T(8,128)} %get-tuple-element.132), channel_id=1, source_target_pairs={{0,1},{1,0},{2,3},{3,2},{4,5},{5,4},{6,7},{7,6},{8,9},{9,8},{10,11... | collective-permute-start | bytes 12582920 | tf_op jit(solution)/shard_map/ppermute | solution.py:208
  408.6 43.2 %collective-permute-start.87 = (f32[2,128,1024]{2,1,0:T(8,128)S(1)}, f32[2,128,1024]{2,1,0:T(8,128)S(1)}, u32[]{:S(2)}, u32[]{:S(2)}) collective-permute-start(f32[2,128,1024]{2,1,0:T(8,128)S(1)} %get-tuple-element.133), channel_id=1, source_target_pairs={{0,2},{1,3},{2,0},{3,1},{4,6},{5,7},{6,4},{7,5},{8,10},{9,11},{10,... | collective-permute-start | bytes 3145736 | tf_op jit(solution)/shard_map/ppermute | solution.py:208
  409.3 45.6 %collective-permute-start.88 = (f32[2,128,1024]{2,1,0:T(8,128)S(1)}, f32[2,128,1024]{2,1,0:T(8,128)S(1)}, u32[]{:S(2)}, u32[]{:S(2)}) collective-permute-start(f32[2,128,1024]{2,1,0:T(8,128)S(1)} %get-tuple-element.134), channel_id=1, source_target_pairs={{0,4},{1,5},{2,6},{3,7},{4,0},{5,1},{6,2},{7,3},{8,12},{9,13},{10,... | collective-permute-start | bytes 3145736 | tf_op jit(solution)/shard_map/ppermute | solution.py:208
  413.8 60.5 %collective-permute-start.82 = (f32[2,128,1024]{2,1,0:T(8,128)S(1)}, f32[2,128,1024]{2,1,0:T(8,128)S(1)}, u32[]{:S(2)}, u32[]{:S(2)}) collective-permute-start(f32[2,128,1024]{2,1,0:T(8,128)S(1)} %get-tuple-element.111), channel_id=1, source_target_pairs={{0,2},{1,3},{2,0},{3,1},{4,6},{5,7},{6,4},{7,5},{8,10},{9,11},{10,... | collective-permute-start | bytes 3145736 | tf_op jit(solution)/shard_map/ppermute | solution.py:208
  429.4 46.4 %collective-permute-start.83 = (f32[2,128,1024]{2,1,0:T(8,128)S(1)}, f32[2,128,1024]{2,1,0:T(8,128)S(1)}, u32[]{:S(2)}, u32[]{:S(2)}) collective-permute-start(f32[2,128,1024]{2,1,0:T(8,128)S(1)} %get-tuple-element.112), channel_id=1, source_target_pairs={{0,4},{1,5},{2,6},{3,7},{4,0},{5,1},{6,2},{7,3},{8,12},{9,13},{10,... | collective-permute-start | bytes 3145736 | tf_op jit(solution)/shard_map/ppermute | solution.py:208
  430.9 65.9 %collective-permute-start.77 = (f32[2,128,1024]{2,1,0:T(8,128)S(1)}, f32[2,128,1024]{2,1,0:T(8,128)S(1)}, u32[]{:S(2)}, u32[]{:S(2)}) collective-permute-start(f32[2,128,1024]{2,1,0:T(8,128)S(1)} %get-tuple-element.105), channel_id=1, source_target_pairs={{0,2},{1,3},{2,0},{3,1},{4,6},{5,7},{6,4},{7,5},{8,10},{9,11},{10,... | collective-permute-start | bytes 3145736 | tf_op jit(solution)/shard_map/ppermute | solution.py:208
  451.8 46.7 %collective-permute-start.78 = (f32[2,128,1024]{2,1,0:T(8,128)S(1)}, f32[2,128,1024]{2,1,0:T(8,128)S(1)}, u32[]{:S(2)}, u32[]{:S(2)}) collective-permute-start(f32[2,128,1024]{2,1,0:T(8,128)S(1)} %get-tuple-element.106), channel_id=1, source_target_pairs={{0,4},{1,5},{2,6},{3,7},{4,0},{5,1},{6,2},{7,3},{8,12},{9,13},{10,... | collective-permute-start | bytes 3145736 | tf_op jit(solution)/shard_map/ppermute | solution.py:208
  454.9 54.6 %collective-permute-start.94 = (f32[1,128,1024]{2,1,0:T(8,128)S(1)}, f32[1,128,1024]{2,1,0:T(8,128)S(1)}, u32[]{:S(2)}, u32[]{:S(2)}) collective-permute-start(f32[1,128,1024]{2,1,0:T(8,128)S(1)} %get-tuple-element.141), channel_id=1, source_target_pairs={{0,4},{1,5},{2,6},{3,7},{4,0},{5,1},{6,2},{7,3},{8,12},{9,13},{10,... | collective-permute-start | bytes 1572872 | tf_op jit(solution)/shard_map/ppermute | solution.py:208
  474.3 35.7 %collective-permute-start.95 = (f32[1,128,1024]{2,1,0:T(8,128)S(1)}, f32[1,128,1024]{2,1,0:T(8,128)S(1)}, u32[]{:S(2)}, u32[]{:S(2)}) collective-permute-start(f32[1,128,1024]{2,1,0:T(8,128)S(1)} %get-tuple-element.142), channel_id=1, source_target_pairs={{0,2},{1,3},{2,0},{3,1},{4,6},{5,7},{6,4},{7,5},{8,10},{9,11},{10,... | collective-permute-start | bytes 1572872 | tf_op jit(solution)/shard_map/ppermute | solution.py:208
  475.8 44.9 %collective-permute-start.89 = (f32[1,128,1024]{2,1,0:T(8,128)S(1)}, f32[1,128,1024]{2,1,0:T(8,128)S(1)}, u32[]{:S(2)}, u32[]{:S(2)}) collective-permute-start(f32[1,128,1024]{2,1,0:T(8,128)S(1)} %get-tuple-element.135), channel_id=1, source_target_pairs={{0,4},{1,5},{2,6},{3,7},{4,0},{5,1},{6,2},{7,3},{8,12},{9,13},{10,... | collective-permute-start | bytes 1572872 | tf_op jit(solution)/shard_map/ppermute | solution.py:208
  498.6 33.4 %collective-permute-start.84 = (f32[1,128,1024]{2,1,0:T(8,128)S(1)}, f32[1,128,1024]{2,1,0:T(8,128)S(1)}, u32[]{:S(2)}, u32[]{:S(2)}) collective-permute-start(f32[1,128,1024]{2,1,0:T(8,128)S(1)} %get-tuple-element.113), channel_id=1, source_target_pairs={{0,4},{1,5},{2,6},{3,7},{4,0},{5,1},{6,2},{7,3},{8,12},{9,13},{10,... | collective-permute-start | bytes 1572872 | tf_op jit(solution)/shard_map/ppermute | solution.py:208
  510.0 32.0 %collective-permute-start.79 = (f32[1,128,1024]{2,1,0:T(8,128)S(1)}, f32[1,128,1024]{2,1,0:T(8,128)S(1)}, u32[]{:S(2)}, u32[]{:S(2)}) collective-permute-start(f32[1,128,1024]{2,1,0:T(8,128)S(1)} %get-tuple-element.107), channel_id=1, source_target_pairs={{0,4},{1,5},{2,6},{3,7},{4,0},{5,1},{6,2},{7,3},{8,12},{9,13},{10,... | collective-permute-start | bytes 1572872 | tf_op jit(solution)/shard_map/ppermute | solution.py:208
  (124 other events, 3093.8 us)
